TPU v7x, 32 devices: a whole 2x2x4 slice. The times are simulated.
32 devices in a mesh: cell: 16 (over z, y, x), gene: 2 (over core).
Axes of the slice: x: 2, y: 2, z: 4, core: 2. Of those that a mesh axis runs over, the one named last changes fastest.
Arguments:
- tiles: bfloat16 [2, 1024, 128, 128], P('gene', 'cell'), may hold values from -8 to 8
- tile_row: int32 [2, 1024], P('gene', 'cell'), may hold values from 0 to 7, as said below
- tile_col: int32 [2, 1024], P('gene', 'cell'), may hold values from 0 to 15
- tile_count: int32 [2, 16], P('gene', 'cell'), may hold values from 1 to 64, as said below
- start_basis: bfloat16 [64, 4096], P(None, 'gene'), may hold values from -0.09375 to 0.09375
Outputs:
- basis: bfloat16 [64, 16384], P(None, 'cell')
- loadings: float32 [64, 4096], P(None, ('gene', 'cell'))
Inputs may be any that keep to these rules, and one draw needn't show every extreme that they name: `tile_row`: tile row of each slot, within 0 to 7; the slots of one device name distinct (row, column) pairs. `tile_count`: slots in use; for each index of gene some device uses all 64.
All inputs are finite; a program needn't handle non-finite values.
Results may differ from a plain program's by a relative error of at most 0.018.
Values may be sent and summed in bfloat16 or wider, within the bound.
No kernel may reach another device: no remote copies, remote signals or barrier semaphores. Data moves between devices by JAX's collectives and lax.ppermute only.
A program may use at most 64 MiB of HBM per device.

v0:
```python
import jax
import jax.numpy as jnp
from jax import lax
from jax.sharding import PartitionSpec as P

ROW_BLOCKS = 8


def solve_lower(lower, right):
    return lax.linalg.triangular_solve(lower, right, left_side=True, lower=True)


def gram_of(scores):
    return jnp.dot(
        scores, scores.T, precision=lax.Precision.HIGHEST, preferred_element_type=jnp.float32
    )


def orthonormal(scores, first_total):
    first = first_total(gram_of(scores))
    lower_one = jnp.linalg.cholesky(first)
    return solve_lower(lower_one, scores)


def local(tiles, tile_row, tile_col, tile_count, start_basis):
    blocks_local = tiles[0]
    slot_count = blocks_local.shape[0]
    tile_size = blocks_local.shape[-1]
    width = start_basis.shape[0]
    gene_dev = start_basis.shape[1]
    gene_blocks = gene_dev // tile_size
    row_blocks = ROW_BLOCKS
    cell_dev = row_blocks * tile_size
    row_index = tile_row[0]
    col_index = tile_col[0]
    live = jnp.arange(slot_count) < tile_count[0, 0]
    row_target = jnp.where(live, row_index, row_blocks)
    col_target = jnp.where(live, col_index, gene_blocks)

    def first_total(gram):
        return lax.psum(gram, ("cell", "gene"))

    def merge_halves(partial_scores):
        return lax.psum_scatter(partial_scores, "gene", scatter_dimension=1, tiled=True)

    def scores_of(basis):
        picked = jnp.take(basis.reshape(width, gene_blocks, tile_size), col_index, axis=1)
        products = jnp.einsum(
            "ksg,srg->skr", picked, blocks_local, preferred_element_type=jnp.float32
        )
        summed = jax.ops.segment_sum(products, row_target, num_segments=row_blocks + 1)[:row_blocks]
        return merge_halves(jnp.transpose(summed, (1, 0, 2)).reshape(width, cell_dev))

    def loadings_of(ortho_half):
        picked = jnp.take(ortho_half.reshape(width, row_blocks, tile_size), row_index, axis=1)
        products = jnp.einsum(
            "ksr,srg->skg", picked, blocks_local, preferred_element_type=jnp.float32
        )
        summed = jax.ops.segment_sum(products, col_target, num_segments=gene_blocks + 1)[
            :gene_blocks
        ]
        return jnp.transpose(summed, (1, 0, 2)).reshape(width, gene_dev)

    ortho = orthonormal(scores_of(start_basis), first_total)
    ortho_half = ortho.astype(jnp.bfloat16)
    ortho_rows = lax.all_gather(ortho_half, "gene", axis=1, tiled=True)
    partial_value = loadings_of(ortho_rows)
    next_basis = lax.psum(partial_value, "cell").astype(jnp.bfloat16)
    ortho_two = orthonormal(scores_of(next_basis), first_total)
    scale = jnp.sqrt(jnp.float32(lax.axis_size("cell") * cell_dev))
    ortho_two_half = ortho_two.astype(jnp.bfloat16)
    basis_piece = (ortho_two * scale).astype(jnp.bfloat16)
    final_rows, basis = (
        lax.all_gather(ortho_two_half, "gene", axis=1, tiled=True),
        lax.all_gather(basis_piece, "gene", axis=1, tiled=True),
    )
    loadings = lax.psum_scatter(loadings_of(final_rows), "cell", scatter_dimension=1, tiled=True)
    return (basis, loadings)


def solution(mesh):
    return jax.shard_map(
        local,
        mesh=mesh,
        in_specs=(
            P("gene", "cell", None, None),
            P("gene", "cell"),
            P("gene", "cell"),
            P("gene", "cell"),
            P(None, "gene"),
        ),
        out_specs=(P(None, "cell"), P(None, ("gene", "cell"))),
        check_vma=False,
    )
```

profile of v0, /device:TPU:0, one launch (start us, length us, event | category | flops | bytes accessed | tf_op | source)
XLA Modules:
  0.0 349.9 jit_solution(15291023441210544630)
XLA Ops:
  7.2 0.8 compare_select_fusion
  8.7 1.0 copy_bitcast_fusion.5
  10.4 0.7 gather_fusion
  11.2 2.9 fusion.6
  14.1 7.1 %scatter_fusion = f32[9,64,128]{2,1,0:T(8,128)S(1)} fusion(f32[9,64,128]{2,1,0:T(8,128)S(1)} %broadcast.69.clone, s32[64]{0:T(128)S(1)} %get-tuple-element.8, f32[64,64,128]{2,1,0:T(8,128)} %fusion.6), kind=kCustom, calls=%fused_computation.4 | custom fusion | flops 524288 | bytes 6291712 | tf_op jit(solution)/shard_map/scatter-add | solution.py:51
  22.0 10.5 %reduce-scatter.4.cloned.1.call-done = f32[64,512]{1,0:T(8,128)} async-done(((f32[64,1024]{1,0:T(8,128)}), f32[64,512]{1,0:T(8,128)}) %reduce-scatter.4.cloned.1.call-update) | async-done | bytes 131088 | tf_op jit(solution)/shard_map/reduce_scatter | solution.py:44
  32.5 1.2 fusion.40
  33.8 40.5 %psum.21 = f32[64,64]{0,1:T(8,128)S(1)} all-reduce(f32[64,64]{0,1:T(8,128)S(1)} %fusion.40), channel_id=1, replica_groups=mesh['cell'=16,'gene'=2] {'cell','gene'}, use_global_device_ids=true, to_apply=%region_2.4 | all-reduce | flops 4096 | bytes 32768 | tf_op jit(solution)/shard_map/psum | solution.py:41
  74.4 5.8 %cholesky.44 = f32[64,64]{1,0:T(8,128)S(1)} custom-call(f32[64,64]{1,0:T(8,128)S(1)} %fusion.30), custom_call_target="Cholesky" | custom-call | tf_op jit(solution)/shard_map/jit(cholesky)/cholesky | solution.py:21
  81.6 4.9 %custom-call.6 = f32[1,64,64]{1,2,0:T(8,128)S(1)} custom-call(f32[1,64,64]{2,1,0:T(8,128)S(1)} %fusion.24), custom_call_target="InvertDiagBlocksLowerTriangular" | custom-call | tf_op jit(solution)/shard_map/triangular_solve/custom-call.0 | solution.py:10
  86.5 1.2 convolution_convert_fusion
  87.7 1.9 all_gather.9
  89.7 0.7 gather_fusion.1
  90.4 2.1 fusion.4
  92.6 7.1 %scatter_fusion.1 = f32[17,64,128]{2,1,0:T(8,128)S(1)} fusion(f32[17,64,128]{2,1,0:T(8,128)S(1)} %broadcast.70.clone, s32[64]{0:T(128)S(1)} %get-tuple-element.9, f32[64,64,128]{2,1,0:T(8,128)} %fusion.4), kind=kCustom, calls=%fused_computation.5 | custom fusion | flops 524288 | bytes 6291712 | tf_op jit(solution)/shard_map/scatter-add | solution.py:59
  99.7 81.7 %all-reduce.1 = bf16[64,2048]{1,0:T(8,128)(2,1)S(1)} all-reduce(f32[64,2048]{1,0:T(8,128)S(1)} %copy_bitcast_fusion.1), channel_id=1, replica_groups=mesh['cell'=16,'gene'=2] {'cell'}, use_global_device_ids=true, to_apply=%region_6.11 | all-reduce | flops 131072 | bytes 786432 | tf_op jit(solution)/shard_map/psum | solution.py:68
  181.4 0.8 gather_fusion.2
  182.2 2.9 fusion.2
  185.1 7.1 %scatter_fusion.2 = f32[9,64,128]{2,1,0:T(8,128)S(1)} fusion(f32[9,64,128]{2,1,0:T(8,128)S(1)} %broadcast.69, s32[64]{0:T(128)S(1)} %get-tuple-element.8, f32[64,64,128]{2,1,0:T(8,128)} %fusion.2), kind=kCustom, calls=%fused_computation.6 | custom fusion | flops 524288 | bytes 6291712 | tf_op jit(solution)/shard_map/scatter-add | solution.py:51
  192.9 4.2 %reduce-scatter.6.cloned.1.call-done = f32[64,512]{1,0:T(8,128)} async-done(((f32[64,1024]{1,0:T(8,128)}), f32[64,512]{1,0:T(8,128)}) %reduce-scatter.6.cloned.1.call-update) | async-done | bytes 131088 | tf_op jit(solution)/shard_map/reduce_scatter | solution.py:44
  197.1 1.2 fusion.41
  198.4 40.8 %psum.23 = f32[64,64]{0,1:T(8,128)S(1)} all-reduce(f32[64,64]{0,1:T(8,128)S(1)} %fusion.41), channel_id=1, replica_groups=mesh['cell'=16,'gene'=2] {'cell','gene'}, use_global_device_ids=true, to_apply=%region_9.14 | all-reduce | flops 4096 | bytes 32768 | tf_op jit(solution)/shard_map/psum | solution.py:41
  239.2 5.8 %cholesky.55 = f32[64,64]{1,0:T(8,128)S(1)} custom-call(f32[64,64]{1,0:T(8,128)S(1)} %fusion.28), custom_call_target="Cholesky" | custom-call | tf_op jit(solution)/shard_map/jit(cholesky)/cholesky | solution.py:21
  246.4 4.9 %custom-call.7 = f32[1,64,64]{1,2,0:T(8,128)S(1)} custom-call(f32[1,64,64]{2,1,0:T(8,128)S(1)} %fusion.25), custom_call_target="InvertDiagBlocksLowerTriangular" | custom-call | tf_op jit(solution)/shard_map/triangular_solve/custom-call.0 | solution.py:10
  251.3 1.2 fusion.39
  252.6 1.9 all_gather.11
  254.5 0.7 gather_fusion.3
  255.2 2.1 fusion
  257.4 7.1 %scatter_fusion.3 = f32[17,64,128]{2,1,0:T(8,128)S(1)} fusion(f32[17,64,128]{2,1,0:T(8,128)S(1)} %broadcast.70, s32[64]{0:T(128)S(1)} %get-tuple-element.9, f32[64,64,128]{2,1,0:T(8,128)} %fusion), kind=kCustom, calls=%fused_computation.7 | custom fusion | flops 524288 | bytes 6291712 | tf_op jit(solution)/shard_map/scatter-add | solution.py:59
  264.4 0.8 copy_bitcast_fusion
  265.3 1.9 all_gather.10
  267.2 75.5 %reduce-scatter.8.cloned.1.call-done = f32[64,128]{1,0:T(8,128)} async-done(((f32[64,2048]{1,0:T(8,128)}), f32[64,128]{1,0:T(8,128)}) %reduce-scatter.8.cloned.1.call-update) | async-done | bytes 32784 | tf_op jit(solution)/shard_map/reduce_scatter | solution.py:77
  (39 shorter events, 6.1 us)
Async XLA Ops:
  7.2 4.0 %copy-start = (bf16[1,64,128,128]{3,2,1,0:T(8,128)(2,1)S(1)}, bf16[1,64,128,128]{3,2,1,0:T(8,128)(2,1)}, u32[]{:S(2)}) copy-start(bf16[1,64,128,128]{3,2,1,0:T(8,128)(2,1)} %param.12) | copy-start | bytes 6291460
  7.2 4.0 %copy-start.1 = (s32[1,64]{1,0:T(1,128)S(1)}, s32[1,64]{1,0:T(1,128)}, u32[]{:S(2)}) copy-start(s32[1,64]{1,0:T(1,128)} %param.14) | copy-start | bytes 772
  7.2 4.0 %copy-start.2 = (s32[1,64]{1,0:T(1,128)S(1)}, s32[1,64]{1,0:T(1,128)}, u32[]{:S(2)}) copy-start(s32[1,64]{1,0:T(1,128)} %param.13) | copy-start | bytes 772
  7.2 25.3 %reduce-scatter.4.cloned.1.call-start = ((), (), s32[]{:S(2)}) async-start(), calls=%async_computation.3 | async-start | bytes 393216 | tf_op jit(solution)/shard_map/reduce_scatter | solution.py:44
  21.9 175.2 %reduce-scatter.6.cloned.1.call-start = ((), (), s32[]{:S(2)}) async-start(), calls=%async_computation.4 | async-start | bytes 393216 | tf_op jit(solution)/shard_map/reduce_scatter | solution.py:44
  192.9 149.8 %reduce-scatter.8.cloned.1.call-start = ((), (), s32[]{:S(2)}) async-start(), calls=%async_computation.5 | async-start | bytes 557056 | tf_op jit(solution)/shard_map/reduce_scatter | solution.py:77
Sparse Core Ops, SparseCore 0:
  22.0 10.4 reduce-scatter.3
  193.0 4.0 reduce-scatter.5
  265.4 77.2 reduce-scatter.7
where the time goes:
time: 351 us; the launch traced here: 350 us
  blocking collectives  169 us (48%)
  waiting for transfers between devices  90.3 us (26%)
  other arithmetic  53.9 us (15%)
  matrix products  14.9 us (4%)
  between operations  14.7 us (4%)
  local copies, waits for them, and re-layouts  7.35 us (2%)
    psum x1, blocking collectives, local(): next_basis = lax.psum(partial_value, 'cell').astype(jnp.bfloat16)  81.7 us
    psum x2, blocking collectives, first_total(): return lax.psum(gram, ('cell', 'gene'))  81.3 us
    reduce_scatter x1, waiting for transfers between devices, local(): lax.psum_scatter(loadings_of(final_rows), 'cell', scatter_dimension=1, ti...  75.5 us
    reduce_scatter x2, waiting for transfers between devices, merge_halves(): lax.psum_scatter(partial_scores, 'gene', scatter_dimension=1, tiled=True)  14.7 us
    scatter-add x2, other arithmetic, scores_of(): jax.ops.segment_sum(products, row_target, num_segments=row_blocks + 1)  14.1 us
    scatter-add x2, other arithmetic, loadings_of(): jax.ops.segment_sum(products, col_target, num_segments=gene_blocks + 1)  14.1 us
    another operation x6, other arithmetic, orthonormal(): lower_one = jnp.linalg.cholesky(first)  13 us
    another operation x4, other arithmetic, solve_lower(): return lax.linalg.triangular_solve(lower, right, left_side=True, lower=True)  11.1 us
  transfers between devices with their start and end apart: 3, of which 3 were waited for; matrix products, arithmetic and copies ran while one was open for 0% of the time, Pallas kernels for 0%

commit v1 on v0

--- a/solution.py
+++ b/solution.py
@@ -4,6 +4,7 @@
 from jax.sharding import PartitionSpec as P
 
 ROW_BLOCKS = 8
+goods_see = lambda along_axis, point, a_name: lax.psum(lax.psum(point, a_name), along_axis)
 
 
 def solve_lower(lower, right):
@@ -38,7 +39,7 @@
     col_target = jnp.where(live, col_index, gene_blocks)
 
     def first_total(gram):
-        return lax.psum(gram, ("cell", "gene"))
+        return goods_see("gene", gram, "cell")
 
     def merge_halves(partial_scores):
         return lax.psum_scatter(partial_scores, "gene", scatter_dimension=1, tiled=True)

time: 351 us -> 425 us (1.21)
  blocking collectives: 169 us -> 244 us
    psum x2 -> x4, blocking collectives: 81.3 us -> 161 us  [the longest x2 154 us: lax.psum(point, a_name)]
    psum x1, blocking collectives: 81.7 us -> 77.3 us  [local(): next_basis = lax.psum(partial_value, 'cell').astype(jnp.bfloat16)]
where the time goes in v1:
time: 425 us; the launch traced here: 423 us
  blocking collectives  244 us (57%)
  waiting for transfers between devices  88.7 us (21%)
  other arithmetic  53.9 us (13%)
  matrix products  14.9 us (4%)
  between operations  14.7 us (3%)
  local copies, waits for them, and re-layouts  7.35 us (2%)
    psum x2, blocking collectives, lax.psum(point, a_name)  154 us
    psum x1, blocking collectives, local(): next_basis = lax.psum(partial_value, 'cell').astype(jnp.bfloat16)  77.3 us
    reduce_scatter x1, waiting for transfers between devices, local(): lax.psum_scatter(loadings_of(final_rows), 'cell', scatter_dimension=1, ti...  72 us
    reduce_scatter x2, waiting for transfers between devices, merge_halves(): lax.psum_scatter(partial_scores, 'gene', scatter_dimension=1, tiled=True)  16.6 us
    scatter-add x2, other arithmetic, scores_of(): jax.ops.segment_sum(products, row_target, num_segments=row_blocks + 1)  14.1 us
    scatter-add x2, other arithmetic, loadings_of(): jax.ops.segment_sum(products, col_target, num_segments=gene_blocks + 1)  14.1 us
    another operation x6, other arithmetic, orthonormal(): lower_one = jnp.linalg.cholesky(first)  13 us
    another operation x4, other arithmetic, solve_lower(): return lax.linalg.triangular_solve(lower, right, left_side=True, lower=True)  11.1 us
  transfers between devices with their start and end apart: 3, of which 3 were waited for; matrix products, arithmetic and copies ran while one was open for 0% of the time, Pallas kernels for 0%

profile of v1, /device:TPU:0, one launch (start us, length us, event | category | flops | bytes accessed | tf_op | source)
XLA Modules:
  0.0 423.5 jit_solution(6048577465296254689)
XLA Ops:
  7.2 0.8 compare_select_fusion
  8.7 1.0 copy_bitcast_fusion.5
  10.4 0.7 gather_fusion
  11.2 2.9 fusion.6
  14.1 7.1 %scatter_fusion = f32[9,64,128]{2,1,0:T(8,128)S(1)} fusion(f32[9,64,128]{2,1,0:T(8,128)S(1)} %broadcast.69.clone, s32[64]{0:T(128)S(1)} %get-tuple-element.8, f32[64,64,128]{2,1,0:T(8,128)} %fusion.6), kind=kCustom, calls=%fused_computation.4 | custom fusion | flops 524288 | bytes 6291712 | tf_op jit(solution)/shard_map/scatter-add | solution.py:52
  22.0 10.5 %reduce-scatter.4.cloned.1.call-done = f32[64,512]{1,0:T(8,128)} async-done(((f32[64,1024]{1,0:T(8,128)}), f32[64,512]{1,0:T(8,128)}) %reduce-scatter.4.cloned.1.call-update) | async-done | bytes 131088 | tf_op jit(solution)/shard_map/reduce_scatter | solution.py:45
  32.5 1.2 fusion.40
  33.8 77.0 %psum.35 = f32[64,64]{0,1:T(8,128)S(1)} all-reduce(f32[64,64]{0,1:T(8,128)S(1)} %fusion.40), channel_id=1, replica_groups=mesh['cell'=16,'gene'=2] {'cell'}, use_global_device_ids=true, to_apply=%region_2.4 | all-reduce | flops 4096 | bytes 32768 | tf_op jit(solution)/shard_map/psum | solution.py:7
  110.7 3.4 psum.36
  114.2 5.8 %cholesky.44 = f32[64,64]{1,0:T(8,128)S(1)} custom-call(f32[64,64]{1,0:T(8,128)S(1)} %fusion.30), custom_call_target="Cholesky" | custom-call | tf_op jit(solution)/shard_map/jit(cholesky)/cholesky | solution.py:22
  121.4 4.9 %custom-call.6 = f32[1,64,64]{1,2,0:T(8,128)S(1)} custom-call(f32[1,64,64]{2,1,0:T(8,128)S(1)} %fusion.24), custom_call_target="InvertDiagBlocksLowerTriangular" | custom-call | tf_op jit(solution)/shard_map/triangular_solve/custom-call.0 | solution.py:11
  126.3 1.2 convolution_convert_fusion
  127.6 1.9 all_gather.9
  130.2 2.1 fusion.4
  132.4 7.1 %scatter_fusion.1 = f32[17,64,128]{2,1,0:T(8,128)S(1)} fusion(f32[17,64,128]{2,1,0:T(8,128)S(1)} %broadcast.70.clone, s32[64]{0:T(128)S(1)} %get-tuple-element.9, f32[64,64,128]{2,1,0:T(8,128)} %fusion.4), kind=kCustom, calls=%fused_computation.5 | custom fusion | flops 524288 | bytes 6291712 | tf_op jit(solution)/shard_map/scatter-add | solution.py:60
  139.5 77.3 %all-reduce.1 = bf16[64,2048]{1,0:T(8,128)(2,1)S(1)} all-reduce(f32[64,2048]{1,0:T(8,128)S(1)} %copy_bitcast_fusion.1), channel_id=1, replica_groups=mesh['cell'=16,'gene'=2] {'cell'}, use_global_device_ids=true, to_apply=%region_7.12 | all-reduce | flops 131072 | bytes 786432 | tf_op jit(solution)/shard_map/psum | solution.py:69
  216.9 0.8 gather_fusion.2
  217.6 2.9 fusion.2
  220.6 7.1 %scatter_fusion.2 = f32[9,64,128]{2,1,0:T(8,128)S(1)} fusion(f32[9,64,128]{2,1,0:T(8,128)S(1)} %broadcast.69, s32[64]{0:T(128)S(1)} %get-tuple-element.8, f32[64,64,128]{2,1,0:T(8,128)} %fusion.2), kind=kCustom, calls=%fused_computation.6 | custom fusion | flops 524288 | bytes 6291712 | tf_op jit(solution)/shard_map/scatter-add | solution.py:52
  228.4 6.1 %reduce-scatter.6.cloned.1.call-done = f32[64,512]{1,0:T(8,128)} async-done(((f32[64,1024]{1,0:T(8,128)}), f32[64,512]{1,0:T(8,128)}) %reduce-scatter.6.cloned.1.call-update) | async-done | bytes 131088 | tf_op jit(solution)/shard_map/reduce_scatter | solution.py:45
  234.5 1.2 fusion.41
  235.8 77.0 %psum.38 = f32[64,64]{0,1:T(8,128)S(1)} all-reduce(f32[64,64]{0,1:T(8,128)S(1)} %fusion.41), channel_id=1, replica_groups=mesh['cell'=16,'gene'=2] {'cell'}, use_global_device_ids=true, to_apply=%region_10.15 | all-reduce | flops 4096 | bytes 32768 | tf_op jit(solution)/shard_map/psum | solution.py:7
  312.8 3.4 psum.39
  316.3 5.8 %cholesky.55 = f32[64,64]{1,0:T(8,128)S(1)} custom-call(f32[64,64]{1,0:T(8,128)S(1)} %fusion.28), custom_call_target="Cholesky" | custom-call | tf_op jit(solution)/shard_map/jit(cholesky)/cholesky | solution.py:22
  323.4 4.9 %custom-call.7 = f32[1,64,64]{1,2,0:T(8,128)S(1)} custom-call(f32[1,64,64]{2,1,0:T(8,128)S(1)} %fusion.25), custom_call_target="InvertDiagBlocksLowerTriangular" | custom-call | tf_op jit(solution)/shard_map/triangular_solve/custom-call.0 | solution.py:11
  328.3 1.2 fusion.39
  329.6 1.9 all_gather.11
  332.3 2.1 fusion
  334.4 7.1 %scatter_fusion.3 = f32[17,64,128]{2,1,0:T(8,128)S(1)} fusion(f32[17,64,128]{2,1,0:T(8,128)S(1)} %broadcast.70, s32[64]{0:T(128)S(1)} %get-tuple-element.9, f32[64,64,128]{2,1,0:T(8,128)} %fusion), kind=kCustom, calls=%fused_computation.7 | custom fusion | flops 524288 | bytes 6291712 | tf_op jit(solution)/shard_map/scatter-add | solution.py:60
  341.5 0.8 copy_bitcast_fusion
  342.3 1.9 all_gather.10
  344.2 72.0 %reduce-scatter.8.cloned.1.call-done = f32[64,128]{1,0:T(8,128)} async-done(((f32[64,2048]{1,0:T(8,128)}), f32[64,128]{1,0:T(8,128)}) %reduce-scatter.8.cloned.1.call-update) | async-done | bytes 32784 | tf_op jit(solution)/shard_map/reduce_scatter | solution.py:78
  (41 shorter events, 7.6 us)
Async XLA Ops:
  7.2 4.0 copy-start
  7.2 4.0 copy-start.1
  7.2 4.0 copy-start.2
  7.2 25.3 %reduce-scatter.4.cloned.1.call-start = ((), (), s32[]{:S(2)}) async-start(), calls=%async_computation.3 | async-start | bytes 393216 | tf_op jit(solution)/shard_map/reduce_scatter | solution.py:45
  21.9 212.6 %reduce-scatter.6.cloned.1.call-start = ((), (), s32[]{:S(2)}) async-start(), calls=%async_computation.4 | async-start | bytes 393216 | tf_op jit(solution)/shard_map/reduce_scatter | solution.py:45
  228.4 187.9 %reduce-scatter.8.cloned.1.call-start = ((), (), s32[]{:S(2)}) async-start(), calls=%async_computation.5 | async-start | bytes 557056 | tf_op jit(solution)/shard_map/reduce_scatter | solution.py:78
Sparse Core Ops, SparseCore 0:
  22.0 10.4 reduce-scatter.3
  228.5 5.9 reduce-scatter.5
  342.4 73.7 reduce-scatter.7
